TPU v7x, 32 devices: a whole 2x2x4 slice. The times are simulated.
32 devices in a mesh: gx: 16 (over z, x, core), gy: 2 (over y).
Axes of the slice: x: 2, y: 2, z: 4, core: 2. Of those that a mesh axis runs over, the one named last changes fastest.
Arguments:
- temp_adjoint: float32 [8, 256, 2048], P(None, 'gy', 'gx'), may hold values from -6 to 6
- height_adjoint: float32 [256, 2048], P('gy', 'gx'), may hold values from -6 to 6
- east_velocity: float32 [8, 256, 2048], P(None, 'gy', 'gx'), may hold values from -0.8 to 0.8
- north_velocity: float32 [8, 256, 2048], P(None, 'gy', 'gx'), may hold values from -0.8 to 0.8
- temp_store: float32 [8, 256, 2048], P(None, 'gy', 'gx'), may hold values from -4 to 4
- salt_store: float32 [8, 256, 2048], P(None, 'gy', 'gx'), may hold values from -4 to 4
- slot_map: int32 [16, 2, 8], P('gx', 'gy'), may hold values from 0 to 7, each once within a row
- land_mask: int32 [8, 256, 2048], P(None, 'gy', 'gx'), may hold values 0 or 1
- ocean_depth: float32 [256, 2048], P('gy', 'gx'), may hold values from 0.1 to 1
Outputs:
- temp_back: float32 [8, 256, 2048], P(None, 'gy', 'gx')
- salt_back: float32 [8, 256, 2048], P(None, 'gy', 'gx')
- surface_adjoint: float32 [256, 2048], P('gy', 'gx')
Inputs may be any that keep to these rules, and one draw needn't show every extreme that they name: `slot_map`: each tile's entries over the last dimension name every slot 0 to 7 once.
All inputs are finite; a program needn't handle non-finite values. No bound on the sum of `land_mask` on one device may be relied on, other than what follows from the above.
Results may differ from a plain program's by a relative error of at most 0.00013.
Values sent between devices are 32-bit elements; how exact they have to be, the bound alone decides.
No kernel may reach another device: no remote copies, remote signals or barrier semaphores. Data moves between devices by JAX's collectives and lax.ppermute only.
A program may use at most 64 MiB of HBM per device.

v0:
```python
import jax
import jax.numpy as jnp
from jax import lax
from jax.sharding import PartitionSpec as P

ITERS = 6
DIFFUSE = 0.2
TIMESTEP = 1.0
STIFFNESS = 8.0
GRAVITY = 4.0
THERMAL = 0.5
NONLINEAR = 0.4
CABBELING = 0.3
HALINE = 0.8


def padded_2(block, sides, width):
    for axis, dim in sides:
        count = lax.axis_size(axis)
        forward = [(i, i + 1) for i in range(count - 1)]
        forward.append((count - 1, 0))
        backward = [(target, source) for source, target in forward]
        low = lax.ppermute(
            lax.slice_in_dim(block, block.shape[dim] - width, None, axis=dim), axis, forward
        )
        high = lax.ppermute(lax.slice_in_dim(block, 0, width, axis=dim), axis, backward)
        block = jnp.concatenate([low, block, high], axis=dim)
    return block


def shifted(value, axis, steps):
    count = lax.axis_size(axis)
    pairs = [(source, (source + steps) % count) for source in range(count)]
    return lax.ppermute(value, axis, pairs)


def clear_walls(padded, row_axis):
    row_index = lax.broadcasted_iota(jnp.int32, padded.shape, row_axis)
    row_count = padded.shape[row_axis]
    lower_wall = (row_index == 0) & (lax.axis_index("gy") == 0)
    upper_wall = (row_index == row_count - 1) & (lax.axis_index("gy") == lax.axis_size("gy") - 1)
    return jnp.where(lower_wall | upper_wall, jnp.zeros_like(padded), padded)


def side_cells(padded):
    return (
        padded[..., 1:-1, :-2],
        padded[..., 1:-1, 2:],
        padded[..., :-2, 1:-1],
        padded[..., 2:, 1:-1],
    )


def surface_apply(grid_field, face_weights):
    padded = padded_2(grid_field, (("gx", 1), ("gy", 0)), 1)
    applied = grid_field
    for face_weight, nearby in zip(face_weights, side_cells(padded)):
        applied = applied + face_weight * (grid_field - nearby)
    return applied


def paired(residual, image_field):
    return lax.psum((jnp.sum(residual * residual), jnp.sum(residual * image_field)), ("gx", "gy"))


def body(
    temp_adjoint,
    height_adjoint,
    east_velocity,
    north_velocity,
    temp_store,
    salt_store,
    slot_map,
    land_mask,
    ocean_depth,
):
    half_cycle = lax.axis_size("gx") // 2
    slot_order = slot_map.reshape(-1)
    both_states = jnp.take(jnp.stack((temp_store, salt_store)), slot_order, axis=1)
    fetched = shifted(both_states, "gx", half_cycle)
    wet_cells = land_mask.astype(jnp.float32)
    masked = wet_cells * temp_adjoint
    east_coef = DIFFUSE - 0.5 * east_velocity
    west_coef = DIFFUSE + 0.5 * east_velocity
    north_coef = DIFFUSE - 0.5 * north_velocity
    south_coef = DIFFUSE + 0.5 * north_velocity
    stacked = jnp.stack((masked, east_velocity, north_velocity))
    padded = padded_2(stacked, (("gx", 3), ("gy", 2)), 1)
    padded = clear_walls(padded, 2)
    mask_west, mask_east, mask_south, mask_north = side_cells(padded[0])
    speed_west, speed_east, _, _ = side_cells(padded[1])
    _, _, speed_south, speed_north = side_cells(padded[2])
    inflow = (DIFFUSE - 0.5 * speed_west) * mask_west + (DIFFUSE + 0.5 * speed_east) * mask_east
    inflow = (
        inflow
        + (DIFFUSE - 0.5 * speed_south) * mask_south
        + (DIFFUSE + 0.5 * speed_north) * mask_north
    )
    tracer_back = masked + TIMESTEP * (
        inflow - (east_coef + west_coef + north_coef + south_coef) * masked
    )
    open_cells = wet_cells[0]
    geometry = padded_2(jnp.stack((open_cells, ocean_depth)), (("gx", 2), ("gy", 1)), 1)
    geometry = clear_walls(geometry, 1)
    face_links = [open_cells * nearby for nearby in side_cells(geometry[0])]
    face_weights = [
        STIFFNESS * 0.5 * (ocean_depth + nearby) * link_open
        for nearby, link_open in zip(side_cells(geometry[1]), face_links)
    ]
    target = open_cells * height_adjoint
    solution = jnp.zeros_like(target)
    residual = target
    image_field = surface_apply(residual, face_weights)
    norm_now, product = paired(residual, image_field)
    step_size = norm_now / product
    direction = residual
    along_dir = image_field
    for iteration in range(ITERS):
        solution = solution + step_size * direction
        if iteration + 1 < ITERS:
            residual = residual - step_size * along_dir
            image_field = surface_apply(residual, face_weights)
            norm_next, product = paired(residual, image_field)
            growth = norm_next / norm_now
            step_size = norm_next / (product - growth * norm_next / step_size)
            direction = residual + growth * direction
            along_dir = image_field + growth * along_dir
            norm_now = norm_next
    height_load = ocean_depth * solution
    load_padded = padded_2(height_load, (("gx", 1), ("gy", 0)), 1)
    pressure_pull = jnp.zeros_like(height_load)
    for link_open, nearby in zip(face_links, side_cells(load_padded)):
        pressure_pull = pressure_pull + link_open * (nearby - height_load)
    adj_pressure = -GRAVITY * pressure_pull
    levels = temp_adjoint.shape[0]
    thickness = 1.0 + jnp.arange(levels, dtype=jnp.float32) / levels
    adj_density = thickness[:, None, None] * adj_pressure[None] * wet_cells
    ck_temp = fetched[0]
    ck_salt = fetched[1]
    temp_back = (
        tracer_back + (THERMAL + 2.0 * NONLINEAR * ck_temp + CABBELING * ck_salt) * adj_density
    )
    salt_back = (HALINE + CABBELING * ck_temp) * adj_density
    return (temp_back, salt_back, solution)


def solution(mesh):
    return jax.shard_map(
        body,
        mesh=mesh,
        in_specs=(
            P(None, "gy", "gx"),
            P("gy", "gx"),
            P(None, "gy", "gx"),
            P(None, "gy", "gx"),
            P(None, "gy", "gx"),
            P(None, "gy", "gx"),
            P("gx", "gy", None),
            P(None, "gy", "gx"),
            P("gy", "gx"),
        ),
        out_specs=(P(None, "gy", "gx"), P(None, "gy", "gx"), P("gy", "gx")),
        check_vma=False,
    )
```

profile of v0, /device:TPU:0, one launch (start us, length us, event | category | flops | bytes accessed | tf_op | source)
XLA Modules:
  0.0 398.7 jit_solution(17863209742963054110)
XLA Ops:
  3.5 5.0 %collective-permute-start.6 = (f32[2,128,1]{2,1,0:T(8,128)S(1)}, f32[2,128,1]{2,1,0:T(8,128)S(1)}, u32[]{:S(2)}, u32[]{:S(2)}) collective-permute-start(f32[2,128,1]{2,1,0:T(8,128)S(1)} %get-tuple-element.68), channel_id=1, source_target_pairs={{2,0},{4,2},{6,4},{8,6},{10,8},{12,10},{14,12},{16,14},{18,16},{20... | collective-permute-start | bytes 3080 | tf_op jit(solution)/shard_map/ppermute | solution.py:26
  9.3 1.9 collective-permute-done.5
  11.3 2.1 collective-permute-start.7
  13.4 2.3 collective-permute-done.9
  15.8 1.5 collective-permute-start.11
  18.1 1.3 collective-permute-done.11
  19.3 1.5 collective-permute-done.12
  21.7 37.1 %all-reduce.5 = (f32[]{:T(128)}, f32[]{:T(128)}) all-reduce(f32[]{:T(128)} %get-tuple-element.14, f32[]{:T(128)} %get-tuple-element.13), channel_id=1, replica_groups=mesh['gx'=16,'gy'=2] {'gx','gy'}, use_global_device_ids=true, to_apply=%region_1.2 | all-reduce | flops 2 | bytes 16 | tf_op jit(solution)/shard_map/psum | solution.py:63
  60.3 4.4 %collective-permute-start.14 = (f32[128,1]{1,0:T(8,128)S(1)}, f32[128,1]{1,0:T(8,128)S(1)}, u32[]{:S(2)}, u32[]{:S(2)}) collective-permute-start(f32[128,1]{1,0:T(8,128)S(1)} %get-tuple-element.80), channel_id=1, source_target_pairs={{2,0},{4,2},{6,4},{8,6},{10,8},{12,10},{14,12},{16,14},{18,16},{20... | collective-permute-start | bytes 1544 | tf_op jit(solution)/shard_map/ppermute | solution.py:26
  64.8 2.0 collective-permute-done.13
  66.9 2.4 collective-permute-start.15
  69.3 1.5 collective-permute-done.15
  70.8 2.0 collective-permute-done.16
  73.7 39.1 %all-reduce.4 = (f32[]{:T(128)}, f32[]{:T(128)}) all-reduce(f32[]{:T(128)} %get-tuple-element.12, f32[]{:T(128)} %get-tuple-element.11), channel_id=1, replica_groups=mesh['gx'=16,'gy'=2] {'gx','gy'}, use_global_device_ids=true, to_apply=%region_5.6 | all-reduce | flops 2 | bytes 16 | tf_op jit(solution)/shard_map/psum | solution.py:63
  117.5 4.4 %collective-permute-start.18 = (f32[128,1]{1,0:T(8,128)S(1)}, f32[128,1]{1,0:T(8,128)S(1)}, u32[]{:S(2)}, u32[]{:S(2)}) collective-permute-start(f32[128,1]{1,0:T(8,128)S(1)} %get-tuple-element.78), channel_id=1, source_target_pairs={{2,0},{4,2},{6,4},{8,6},{10,8},{12,10},{14,12},{16,14},{18,16},{20... | collective-permute-start | bytes 1544 | tf_op jit(solution)/shard_map/ppermute | solution.py:26
  122.0 2.0 collective-permute-done.17
  124.0 2.4 collective-permute-start.19
  126.7 1.3 collective-permute-done.19
  128.0 2.0 collective-permute-done.20
  130.8 37.5 %all-reduce.3 = (f32[]{:T(128)}, f32[]{:T(128)}) all-reduce(f32[]{:T(128)} %get-tuple-element.10, f32[]{:T(128)} %get-tuple-element.9), channel_id=1, replica_groups=mesh['gx'=16,'gy'=2] {'gx','gy'}, use_global_device_ids=true, to_apply=%region_9.10 | all-reduce | flops 2 | bytes 16 | tf_op jit(solution)/shard_map/psum | solution.py:63
  172.7 4.4 %collective-permute-start.22 = (f32[128,1]{1,0:T(8,128)}, f32[128,1]{1,0:T(8,128)S(1)}, u32[]{:S(2)}, u32[]{:S(2)}) collective-permute-start(f32[128,1]{1,0:T(8,128)} %get-tuple-element.76), channel_id=1, source_target_pairs={{2,0},{4,2},{6,4},{8,6},{10,8},{12,10},{14,12},{16,14},{18,16},{20... | collective-permute-start | bytes 1544 | tf_op jit(solution)/shard_map/ppermute | solution.py:26
  177.1 2.2 fusion.119
  179.3 2.0 copy.15
  181.8 4.4 %collective-permute-start.1 = (f32[3,8,128,1]{2,1,3,0:T(8,128)S(1)}, f32[3,8,128,1]{2,1,3,0:T(8,128)}, u32[]{:S(2)}, u32[]{:S(2)}) collective-permute-start(f32[3,8,128,1]{2,1,3,0:T(8,128)S(1)} %copy.16), channel_id=1, source_target_pairs={{2,0},{4,2},{6,4},{8,6},{10,8},{12,10},{14,12},{16,14},{18,16},{20... | collective-permute-start | bytes 36872 | tf_op jit(solution)/shard_map/ppermute | solution.py:26
  186.3 2.5 collective-permute-start.23
  188.9 1.5 collective-permute-done.23
  190.4 2.0 collective-permute-done.24
  192.4 1.7 multiply_reduce_fusion.3
  194.1 37.1 %all-reduce.2 = (f32[]{:T(128)}, f32[]{:T(128)}) all-reduce(f32[]{:T(128)} %get-tuple-element.8, f32[]{:T(128)} %get-tuple-element.7), channel_id=1, replica_groups=mesh['gx'=16,'gy'=2] {'gx','gy'}, use_global_device_ids=true, to_apply=%region_13.14 | all-reduce | flops 2 | bytes 16 | tf_op jit(solution)/shard_map/psum | solution.py:63
  235.2 4.4 %collective-permute-start.26 = (f32[128,1]{1,0:T(8,128)S(1)}, f32[128,1]{1,0:T(8,128)S(1)}, u32[]{:S(2)}, u32[]{:S(2)}) collective-permute-start(f32[128,1]{1,0:T(8,128)S(1)} %get-tuple-element.74), channel_id=1, source_target_pairs={{2,0},{4,2},{6,4},{8,6},{10,8},{12,10},{14,12},{16,14},{18,16},{20... | collective-permute-start | bytes 1544 | tf_op jit(solution)/shard_map/ppermute | solution.py:26
  239.6 2.0 collective-permute-done.25
  241.7 2.4 collective-permute-start.27
  244.3 1.3 pad_maximum_fusion.1
  245.7 2.0 collective-permute-done.28
  248.6 39.1 %all-reduce.1 = (f32[]{:T(128)}, f32[]{:T(128)}) all-reduce(f32[]{:T(128)} %get-tuple-element.6, f32[]{:T(128)} %get-tuple-element.5), channel_id=1, replica_groups=mesh['gx'=16,'gy'=2] {'gx','gy'}, use_global_device_ids=true, to_apply=%region_17.18 | all-reduce | flops 2 | bytes 16 | tf_op jit(solution)/shard_map/psum | solution.py:63
  291.9 4.4 %collective-permute-start.30 = (f32[128,1]{1,0:T(8,128)S(1)}, f32[128,1]{1,0:T(8,128)S(1)}, u32[]{:S(2)}, u32[]{:S(2)}) collective-permute-start(f32[128,1]{1,0:T(8,128)S(1)} %get-tuple-element.72), channel_id=1, source_target_pairs={{2,0},{4,2},{6,4},{8,6},{10,8},{12,10},{14,12},{16,14},{18,16},{20... | collective-permute-start | bytes 1544 | tf_op jit(solution)/shard_map/ppermute | solution.py:26
  297.0 1.4 collective-permute-done.29
  298.5 2.4 collective-permute-start.31
  302.5 2.0 collective-permute-done.32
  305.3 63.6 %all-reduce = (f32[]{:T(128)}, f32[]{:T(128)}) all-reduce(f32[]{:T(128)} %get-tuple-element.4, f32[]{:T(128)} %get-tuple-element.3), channel_id=1, replica_groups=mesh['gx'=16,'gy'=2] {'gx','gy'}, use_global_device_ids=true, to_apply=%region_21.22 | all-reduce | flops 2 | bytes 16 | tf_op jit(solution)/shard_map/psum | solution.py:63
  374.0 4.4 %collective-permute-start.34 = (f32[128,1]{1,0:T(8,128)S(1)}, f32[128,1]{1,0:T(8,128)S(1)}, u32[]{:S(2)}, u32[]{:S(2)}) collective-permute-start(f32[128,1]{1,0:T(8,128)S(1)} %get-tuple-element.70), channel_id=1, source_target_pairs={{2,0},{4,2},{6,4},{8,6},{10,8},{12,10},{14,12},{16,14},{18,16},{20... | collective-permute-start | bytes 1544 | tf_op jit(solution)/shard_map/ppermute | solution.py:26
  378.4 2.0 collective-permute-done.33
  380.5 2.4 collective-permute-start.35
  383.6 1.2 copy.18
  386.0 2.0 collective-permute-start.2
  389.9 1.9 collective-permute-done.3
  391.8 2.3 maximum_select_fusion
  395.4 3.3 bitcast_multiply_fusion
  (117 shorter events, 19.5 us)
Async XLA Ops:
  0.6 10.6 %copy-start.11 = (f32[128,128]{1,0:T(8,128)S(1)}, f32[128,128]{1,0:T(8,128)}, u32[]{:S(2)}) copy-start(f32[128,128]{1,0:T(8,128)} %param.17) | copy-start | bytes 196612
  0.6 7.9 %copy-start.14 = (f32[128,128]{1,0:T(8,128)S(1)}, f32[128,128]{1,0:T(8,128)}, u32[]{:S(2)}) copy-start(f32[128,128]{1,0:T(8,128)} %param.10) | copy-start | bytes 196612
  1.8 20.0 %copy-start.12 = (f32[8,128,128]{2,1,0:T(8,128)}, f32[8,128,128]{2,1,0:T(8,128)S(1)}, u32[]{:S(2)}) copy-start(f32[8,128,128]{2,1,0:T(8,128)S(1)} %convert_element_type.3) | copy-start | bytes 1572868
  2.9 8.3 %collective-permute-start.5 = (f32[2,128,1]{2,1,0:T(8,128)S(1)}, f32[2,128,1]{2,1,0:T(8,128)S(1)}, u32[]{:S(2)}, u32[]{:S(2)}) collective-permute-start(f32[2,128,1]{2,1,0:T(8,128)S(1)} %get-tuple-element.67), channel_id=1, source_target_pairs={{0,2},{2,4},{4,6},{6,8},{8,10},{10,12},{12,14},{14,16},{16,18},{18... | collective-permute-start | bytes 3080 | tf_op jit(solution)/shard_map/ppermute | solution.py:23
  3.5 7.7 %collective-permute-start.6 = (f32[2,128,1]{2,1,0:T(8,128)S(1)}, f32[2,128,1]{2,1,0:T(8,128)S(1)}, u32[]{:S(2)}, u32[]{:S(2)}) collective-permute-start(f32[2,128,1]{2,1,0:T(8,128)S(1)} %get-tuple-element.68), channel_id=1, source_target_pairs={{2,0},{4,2},{6,4},{8,6},{10,8},{12,10},{14,12},{16,14},{18,16},{20... | collective-permute-start | bytes 3080 | tf_op jit(solution)/shard_map/ppermute | solution.py:26
  8.6 4.8 %collective-permute-start.10 = (f32[128,1]{1,0:T(8,128)S(1)}, f32[128,1]{1,0:T(8,128)S(1)}, u32[]{:S(2)}, u32[]{:S(2)}) collective-permute-start(f32[128,1]{1,0:T(8,128)S(1)} %get-tuple-element.82), channel_id=1, source_target_pairs={{2,0},{4,2},{6,4},{8,6},{10,8},{12,10},{14,12},{16,14},{18,16},{20... | collective-permute-start | bytes 1544 | tf_op jit(solution)/shard_map/ppermute | solution.py:26
  9.3 6.4 %collective-permute-start.9 = (f32[128,1]{1,0:T(8,128)S(1)}, f32[128,1]{1,0:T(8,128)S(1)}, u32[]{:S(2)}, u32[]{:S(2)}) collective-permute-start(f32[128,1]{1,0:T(8,128)S(1)} %get-tuple-element.81), channel_id=1, source_target_pairs={{0,2},{2,4},{4,6},{6,8},{8,10},{10,12},{12,14},{14,16},{16,18},{18... | collective-permute-start | bytes 1544 | tf_op jit(solution)/shard_map/ppermute | solution.py:23
  11.3 6.5 %collective-permute-start.7 = (f32[2,1,130]{2,1,0:T(1,128)S(1)}, f32[2,1,130]{2,1,0:T(1,128)S(1)}, u32[]{:S(2)}, u32[]{:S(2)}) collective-permute-start(f32[2,1,130]{2,1,0:T(1,128)S(1)} %get-tuple-element.49), channel_id=1, source_target_pairs={{0,1},{1,0},{2,3},{3,2},{4,5},{5,4},{6,7},{7,6},{8,9},{9,8},{10,11... | collective-permute-start | bytes 3128 | tf_op jit(solution)/shard_map/ppermute | solution.py:23
  13.3 4.5 %collective-permute-start.8 = (f32[2,1,130]{2,1,0:T(1,128)S(1)}, f32[2,1,130]{2,1,0:T(1,128)S(1)}, u32[]{:S(2)}, u32[]{:S(2)}) collective-permute-start(f32[2,1,130]{2,1,0:T(1,128)S(1)} %get-tuple-element.50), channel_id=1, source_target_pairs={{1,0},{0,1},{3,2},{2,3},{5,4},{4,5},{7,6},{6,7},{9,8},{8,9},{11,10... | collective-permute-start | bytes 3128 | tf_op jit(solution)/shard_map/ppermute | solution.py:26
  15.8 3.6 collective-permute-start.11
  17.3 3.6 collective-permute-start.12
  18.0 103.8 %copy-start.7 = (s32[8,128,128]{2,1,0:T(8,128)S(1)}, s32[8,128,128]{2,1,0:T(8,128)}, u32[]{:S(2)}) copy-start(s32[8,128,128]{2,1,0:T(8,128)} %param.16) | copy-start | bytes 1572868
  18.0 103.8 %copy-start.9 = (f32[8,128,128]{2,1,0:T(8,128)S(1)}, f32[8,128,128]{2,1,0:T(8,128)}, u32[]{:S(2)}) copy-start(f32[8,128,128]{2,1,0:T(8,128)} %param.9) | copy-start | bytes 1572868
  60.3 66.3 %copy-start = (f32[8,128,128]{2,1,0:T(8,128)S(1)}, f32[8,128,128]{2,1,0:T(8,128)}, u32[]{:S(2)}) copy-start(f32[8,128,128]{2,1,0:T(8,128)} %param.12) | copy-start | bytes 1572868
  60.3 66.3 %copy-start.2 = (f32[8,128,128]{2,1,0:T(8,128)S(1)}, f32[8,128,128]{2,1,0:T(8,128)}, u32[]{:S(2)}) copy-start(f32[8,128,128]{2,1,0:T(8,128)} %param.11) | copy-start | bytes 1572868
  60.3 6.5 %collective-permute-start.13 = (f32[128,1]{1,0:T(8,128)S(1)}, f32[128,1]{1,0:T(8,128)S(1)}, u32[]{:S(2)}, u32[]{:S(2)}) collective-permute-start(f32[128,1]{1,0:T(8,128)S(1)} %get-tuple-element.79), channel_id=1, source_target_pairs={{0,2},{2,4},{4,6},{6,8},{8,10},{10,12},{12,14},{14,16},{16,18},{18... | collective-permute-start | bytes 1544 | tf_op jit(solution)/shard_map/ppermute | solution.py:23
  60.3 6.5 %collective-permute-start.14 = (f32[128,1]{1,0:T(8,128)S(1)}, f32[128,1]{1,0:T(8,128)S(1)}, u32[]{:S(2)}, u32[]{:S(2)}) collective-permute-start(f32[128,1]{1,0:T(8,128)S(1)} %get-tuple-element.80), channel_id=1, source_target_pairs={{2,0},{4,2},{6,4},{8,6},{10,8},{12,10},{14,12},{16,14},{18,16},{20... | collective-permute-start | bytes 1544 | tf_op jit(solution)/shard_map/ppermute | solution.py:26
  66.9 3.9 collective-permute-start.15
  69.3 3.6 collective-permute-start.16
  117.4 6.5 %collective-permute-start.17 = (f32[128,1]{1,0:T(8,128)S(1)}, f32[128,1]{1,0:T(8,128)S(1)}, u32[]{:S(2)}, u32[]{:S(2)}) collective-permute-start(f32[128,1]{1,0:T(8,128)S(1)} %get-tuple-element.77), channel_id=1, source_target_pairs={{0,2},{2,4},{4,6},{6,8},{8,10},{10,12},{12,14},{14,16},{16,18},{18... | collective-permute-start | bytes 1544 | tf_op jit(solution)/shard_map/ppermute | solution.py:23
  117.5 6.5 %collective-permute-start.18 = (f32[128,1]{1,0:T(8,128)S(1)}, f32[128,1]{1,0:T(8,128)S(1)}, u32[]{:S(2)}, u32[]{:S(2)}) collective-permute-start(f32[128,1]{1,0:T(8,128)S(1)} %get-tuple-element.78), channel_id=1, source_target_pairs={{2,0},{4,2},{6,4},{8,6},{10,8},{12,10},{14,12},{16,14},{18,16},{20... | collective-permute-start | bytes 1544 | tf_op jit(solution)/shard_map/ppermute | solution.py:26
  124.0 4.0 %collective-permute-start.19 = (f32[1,130]{1,0:T(1,128)S(1)}, f32[1,130]{1,0:T(1,128)S(1)}, u32[]{:S(2)}, u32[]{:S(2)}) collective-permute-start(f32[1,130]{1,0:T(1,128)S(1)} %get-tuple-element.61), channel_id=1, source_target_pairs={{0,1},{1,0},{2,3},{3,2},{4,5},{5,4},{6,7},{7,6},{8,9},{9,8},{10,11... | collective-permute-start | bytes 1568 | tf_op jit(solution)/shard_map/ppermute | solution.py:23
  126.4 3.6 collective-permute-start.20
  172.7 13.6 %collective-permute-start.21 = (f32[128,1]{1,0:T(8,128)}, f32[128,1]{1,0:T(8,128)S(1)}, u32[]{:S(2)}, u32[]{:S(2)}) collective-permute-start(f32[128,1]{1,0:T(8,128)} %get-tuple-element.75), channel_id=1, source_target_pairs={{0,2},{2,4},{4,6},{6,8},{8,10},{10,12},{12,14},{14,16},{16,18},{18... | collective-permute-start | bytes 1544 | tf_op jit(solution)/shard_map/ppermute | solution.py:23
  172.7 13.6 %collective-permute-start.22 = (f32[128,1]{1,0:T(8,128)}, f32[128,1]{1,0:T(8,128)S(1)}, u32[]{:S(2)}, u32[]{:S(2)}) collective-permute-start(f32[128,1]{1,0:T(8,128)} %get-tuple-element.76), channel_id=1, source_target_pairs={{2,0},{4,2},{6,4},{8,6},{10,8},{12,10},{14,12},{16,14},{18,16},{20... | collective-permute-start | bytes 1544 | tf_op jit(solution)/shard_map/ppermute | solution.py:26
  179.3 9.6 %copy-start.15 = (s32[1,1,8]{2,1,0:T(1,128)S(1)}, s32[1,1,8]{2,1,0:T(1,128)}, u32[]{:S(2)}) copy-start(s32[1,1,8]{2,1,0:T(1,128)} %param.15) | copy-start | bytes 100
  181.3 201.8 %collective-permute-start = (f32[3,8,128,1]{2,1,3,0:T(8,128)S(1)}, f32[3,8,128,1]{2,1,3,0:T(8,128)S(1)}, u32[]{:S(2)}, u32[]{:S(2)}) collective-permute-start(f32[3,8,128,1]{2,1,3,0:T(8,128)S(1)} %copy.15), channel_id=1, source_target_pairs={{0,2},{2,4},{4,6},{6,8},{8,10},{10,12},{12,14},{14,16},{16,18},{18... | collective-permute-start | bytes 36872 | tf_op jit(solution)/shard_map/ppermute | solution.py:23
  181.8 201.8 %collective-permute-start.1 = (f32[3,8,128,1]{2,1,3,0:T(8,128)S(1)}, f32[3,8,128,1]{2,1,3,0:T(8,128)}, u32[]{:S(2)}, u32[]{:S(2)}) collective-permute-start(f32[3,8,128,1]{2,1,3,0:T(8,128)S(1)} %copy.16), channel_id=1, source_target_pairs={{2,0},{4,2},{6,4},{8,6},{10,8},{12,10},{14,12},{16,14},{18,16},{20... | collective-permute-start | bytes 36872 | tf_op jit(solution)/shard_map/ppermute | solution.py:26
  186.3 4.0 %collective-permute-start.23 = (f32[1,130]{1,0:T(1,128)S(1)}, f32[1,130]{1,0:T(1,128)S(1)}, u32[]{:S(2)}, u32[]{:S(2)}) collective-permute-start(f32[1,130]{1,0:T(1,128)S(1)} %get-tuple-element.59), channel_id=1, source_target_pairs={{0,1},{1,0},{2,3},{3,2},{4,5},{5,4},{6,7},{7,6},{8,9},{9,8},{10,11... | collective-permute-start | bytes 1568 | tf_op jit(solution)/shard_map/ppermute | solution.py:23
  188.8 3.6 collective-permute-start.24
  235.1 6.5 %collective-permute-start.25 = (f32[128,1]{1,0:T(8,128)S(1)}, f32[128,1]{1,0:T(8,128)S(1)}, u32[]{:S(2)}, u32[]{:S(2)}) collective-permute-start(f32[128,1]{1,0:T(8,128)S(1)} %get-tuple-element.73), channel_id=1, source_target_pairs={{0,2},{2,4},{4,6},{6,8},{8,10},{10,12},{12,14},{14,16},{16,18},{18... | collective-permute-start | bytes 1544 | tf_op jit(solution)/shard_map/ppermute | solution.py:23
  235.2 6.5 %collective-permute-start.26 = (f32[128,1]{1,0:T(8,128)S(1)}, f32[128,1]{1,0:T(8,128)S(1)}, u32[]{:S(2)}, u32[]{:S(2)}) collective-permute-start(f32[128,1]{1,0:T(8,128)S(1)} %get-tuple-element.74), channel_id=1, source_target_pairs={{2,0},{4,2},{6,4},{8,6},{10,8},{12,10},{14,12},{16,14},{18,16},{20... | collective-permute-start | bytes 1544 | tf_op jit(solution)/shard_map/ppermute | solution.py:26
  241.7 4.0 %collective-permute-start.27 = (f32[1,130]{1,0:T(1,128)S(1)}, f32[1,130]{1,0:T(1,128)S(1)}, u32[]{:S(2)}, u32[]{:S(2)}) collective-permute-start(f32[1,130]{1,0:T(1,128)S(1)} %get-tuple-element.57), channel_id=1, source_target_pairs={{0,1},{1,0},{2,3},{3,2},{4,5},{5,4},{6,7},{7,6},{8,9},{9,8},{10,11... | collective-permute-start | bytes 1568 | tf_op jit(solution)/shard_map/ppermute | solution.py:23
  244.2 3.6 collective-permute-start.28
  291.9 6.5 %collective-permute-start.29 = (f32[128,1]{1,0:T(8,128)S(1)}, f32[128,1]{1,0:T(8,128)S(1)}, u32[]{:S(2)}, u32[]{:S(2)}) collective-permute-start(f32[128,1]{1,0:T(8,128)S(1)} %get-tuple-element.71), channel_id=1, source_target_pairs={{0,2},{2,4},{4,6},{6,8},{8,10},{10,12},{12,14},{14,16},{16,18},{18... | collective-permute-start | bytes 1544 | tf_op jit(solution)/shard_map/ppermute | solution.py:23
  291.9 6.5 %collective-permute-start.30 = (f32[128,1]{1,0:T(8,128)S(1)}, f32[128,1]{1,0:T(8,128)S(1)}, u32[]{:S(2)}, u32[]{:S(2)}) collective-permute-start(f32[128,1]{1,0:T(8,128)S(1)} %get-tuple-element.72), channel_id=1, source_target_pairs={{2,0},{4,2},{6,4},{8,6},{10,8},{12,10},{14,12},{16,14},{18,16},{20... | collective-permute-start | bytes 1544 | tf_op jit(solution)/shard_map/ppermute | solution.py:26
  298.5 4.0 %collective-permute-start.31 = (f32[1,130]{1,0:T(1,128)S(1)}, f32[1,130]{1,0:T(1,128)S(1)}, u32[]{:S(2)}, u32[]{:S(2)}) collective-permute-start(f32[1,130]{1,0:T(1,128)S(1)} %get-tuple-element.55), channel_id=1, source_target_pairs={{0,1},{1,0},{2,3},{3,2},{4,5},{5,4},{6,7},{7,6},{8,9},{9,8},{10,11... | collective-permute-start | bytes 1568 | tf_op jit(solution)/shard_map/ppermute | solution.py:23
  300.9 3.6 collective-permute-start.32
  302.2 92.3 %collective-permute-start.4 = (f32[2,8,128,128]{3,2,0,1:T(8,128)}, f32[2,8,128,128]{3,2,0,1:T(8,128)}, u32[]{:S(2)}, u32[]{:S(2)}) collective-permute-start(f32[2,8,128,128]{3,2,0,1:T(8,128)} %select_bitcast_fusion), channel_id=1, source_target_pairs={{0,16},{2,18},{4,20},{6,22},{8,24},{10,26},{12,28},{14,30},{16,0},... | collective-permute-start | bytes 3145736 | tf_op jit(solution)/shard_map/ppermute | solution.py:34
  373.9 6.5 %collective-permute-start.33 = (f32[128,1]{1,0:T(8,128)S(1)}, f32[128,1]{1,0:T(8,128)S(1)}, u32[]{:S(2)}, u32[]{:S(2)}) collective-permute-start(f32[128,1]{1,0:T(8,128)S(1)} %get-tuple-element.69), channel_id=1, source_target_pairs={{0,2},{2,4},{4,6},{6,8},{8,10},{10,12},{12,14},{14,16},{16,18},{18... | collective-permute-start | bytes 1544 | tf_op jit(solution)/shard_map/ppermute | solution.py:23
  374.0 6.5 %collective-permute-start.34 = (f32[128,1]{1,0:T(8,128)S(1)}, f32[128,1]{1,0:T(8,128)S(1)}, u32[]{:S(2)}, u32[]{:S(2)}) collective-permute-start(f32[128,1]{1,0:T(8,128)S(1)} %get-tuple-element.70), channel_id=1, source_target_pairs={{2,0},{4,2},{6,4},{8,6},{10,8},{12,10},{14,12},{16,14},{18,16},{20... | collective-permute-start | bytes 1544 | tf_op jit(solution)/shard_map/ppermute | solution.py:26
  380.5 7.6 %collective-permute-start.35 = (f32[1,130]{1,0:T(1,128)S(1)}, f32[1,130]{1,0:T(1,128)S(1)}, u32[]{:S(2)}, u32[]{:S(2)}) collective-permute-start(f32[1,130]{1,0:T(1,128)S(1)} %get-tuple-element.53), channel_id=1, source_target_pairs={{0,1},{1,0},{2,3},{3,2},{4,5},{5,4},{6,7},{7,6},{8,9},{9,8},{10,11... | collective-permute-start | bytes 1568 | tf_op jit(solution)/shard_map/ppermute | solution.py:23
  383.0 5.1 %collective-permute-start.36 = (f32[1,130]{1,0:T(1,128)S(1)}, f32[1,130]{1,0:T(1,128)S(1)}, u32[]{:S(2)}, u32[]{:S(2)}) collective-permute-start(f32[1,130]{1,0:T(1,128)S(1)} %get-tuple-element.54), channel_id=1, source_target_pairs={{1,0},{0,1},{3,2},{2,3},{5,4},{4,5},{7,6},{6,7},{9,8},{8,9},{11,10... | collective-permute-start | bytes 1568 | tf_op jit(solution)/shard_map/ppermute | solution.py:26
  384.8 7.1 %copy-start.1 = (f32[8,128,128]{2,1,0:T(8,128)S(1)}, f32[8,128,128]{2,1,0:T(8,128)}, u32[]{:S(2)}) copy-start(f32[8,128,128]{2,1,0:T(8,128)} %param.12) | copy-start | bytes 1572868
  384.8 7.0 %copy-start.3 = (f32[8,128,128]{2,1,0:T(8,128)S(1)}, f32[8,128,128]{2,1,0:T(8,128)}, u32[]{:S(2)}) copy-start(f32[8,128,128]{2,1,0:T(8,128)} %param.11) | copy-start | bytes 1572868
  384.8 7.0 %copy-start.5 = (f32[1,8,128,128]{3,2,1,0:T(8,128)S(1)}, f32[1,8,128,128]{3,2,1,0:T(8,128)}, u32[]{:S(2)}) copy-start(f32[1,8,128,128]{3,2,1,0:T(8,128)} %copy-done.4) | copy-start | bytes 1572868
  386.0 3.9 collective-permute-start.2
  388.0 3.8 collective-permute-start.3
  (5 other events, 13.1 us)
where the time goes:
time: 400 us; the launch traced here: 399 us
  blocking collectives  253 us (63%)
  starting transfers between devices  58.8 us (15%)
  waiting for transfers between devices  34 us (8%)
  between operations  22.8 us (6%)
  other arithmetic  20.2 us (5%)
  local copies, waits for them, and re-layouts  9.43 us (2%)
    psum x6, blocking collectives, paired(): lax.psum((jnp.sum(residual * residual), jnp.sum(residual * image_field)),...  253 us
    ppermute x18, starting transfers between devices, padded_2(): lax.ppermute(lax.slice_in_dim(block, 0, width, axis=dim), axis, backward)  37.9 us
    ppermute x18, starting transfers between devices, padded_2(): lax.ppermute(lax.slice_in_dim(block, block.shape[dim] - width, None, axis...  21 us
    ppermute x18, waiting for transfers between devices, padded_2(): lax.ppermute(lax.slice_in_dim(block, block.shape[dim] - width, None, axis...  20.4 us
    ppermute x18, waiting for transfers between devices, padded_2(): lax.ppermute(lax.slice_in_dim(block, 0, width, axis=dim), axis, backward)  13.6 us
  transfers between devices with their start and end apart: 37, of which 21 were waited for; matrix products, arithmetic and copies ran while one was open for 5% of the time, Pallas kernels for 0%

commit v1 on v0

--- a/solution.py
+++ b/solution.py
@@ -60,7 +60,13 @@
 
 
 def paired(residual, image_field):
-    return lax.psum((jnp.sum(residual * residual), jnp.sum(residual * image_field)), ("gx", "gy"))
+
+    def create_gates_now(matrix, along_axis, group_axis="gx"):
+        for j0 in (along_axis, group_axis):
+            matrix = lax.psum(matrix, j0)
+        return matrix
+
+    return create_gates_now((jnp.sum(residual * residual), jnp.sum(residual * image_field)), "gy")
 
 
 def body(

time: 400 us -> 374 us (0.935); the launches traced: 399 us -> 367 us
  blocking collectives: 253 us -> 231 us
  waiting for transfers between devices: 34 us -> 27.9 us
    psum x6 -> x12, blocking collectives: 253 us -> 231 us  [create_gates_now(): matrix = lax.psum(matrix, j0)]
    ppermute x18, starting transfers between devices: 21 us -> 13.5 us  [padded_2(): lax.ppermute(lax.slice_in_dim(block, block.shape[dim] - width, None, axis...]
    ppermute x18, waiting for transfers between devices: 13.6 us -> 7.54 us  [padded_2(): lax.ppermute(lax.slice_in_dim(block, 0, width, axis=dim), axis, backward)]
    ppermute x18, starting transfers between devices: 37.9 us -> 42.9 us  [padded_2(): lax.ppermute(lax.slice_in_dim(block, 0, width, axis=dim), axis, backward)]
  transfers between devices with their start and end apart: 37 -> 37, of which waited for: 21 -> 22; matrix products, arithmetic and copies ran while one was open for 5% -> 5% of each run, Pallas kernels for 0% -> 0%
where the time goes in v1:
time: 374 us; the launch traced here: 367 us
  blocking collectives  231 us (62%)
  starting transfers between devices  56.4 us (15%)
  waiting for transfers between devices  27.9 us (7%)
  between operations  22.6 us (6%)
  other arithmetic  20.2 us (5%)
  local copies, waits for them, and re-layouts  9.44 us (3%)
    psum x12, blocking collectives, create_gates_now(): matrix = lax.psum(matrix, j0)  231 us
    ppermute x18, starting transfers between devices, padded_2(): lax.ppermute(lax.slice_in_dim(block, 0, width, axis=dim), axis, backward)  42.9 us
    ppermute x18, waiting for transfers between devices, padded_2(): lax.ppermute(lax.slice_in_dim(block, block.shape[dim] - width, None, axis...  20.3 us
    ppermute x18, starting transfers between devices, padded_2(): lax.ppermute(lax.slice_in_dim(block, block.shape[dim] - width, None, axis...  13.5 us
    ppermute x18, waiting for transfers between devices, padded_2(): lax.ppermute(lax.slice_in_dim(block, 0, width, axis=dim), axis, backward)  7.54 us
  transfers between devices with their start and end apart: 37, of which 22 were waited for; matrix products, arithmetic and copies ran while one was open for 5% of the time, Pallas kernels for 0%

profile of v1, /device:TPU:0, one launch (start us, length us, event | category | flops | bytes accessed | tf_op | source)
XLA Modules:
  0.0 367.1 jit_solution(5566582060140123170)
XLA Ops:
  3.5 5.0 %collective-permute-start.6 = (f32[2,128,1]{2,1,0:T(8,128)S(1)}, f32[2,128,1]{2,1,0:T(8,128)S(1)}, u32[]{:S(2)}, u32[]{:S(2)}) collective-permute-start(f32[2,128,1]{2,1,0:T(8,128)S(1)} %get-tuple-element.80), channel_id=1, source_target_pairs={{2,0},{4,2},{6,4},{8,6},{10,8},{12,10},{14,12},{16,14},{18,16},{20... | collective-permute-start | bytes 3080 | tf_op jit(solution)/shard_map/ppermute | solution.py:26
  9.3 1.9 collective-permute-done.5
  11.3 2.1 collective-permute-start.7
  13.4 2.3 collective-permute-done.9
  15.8 1.5 collective-permute-start.11
  19.3 1.5 collective-permute-done.12
  21.7 5.5 %all-reduce.11 = (f32[]{:T(128)}, f32[]{:T(128)}) all-reduce(f32[]{:T(128)} %get-tuple-element.14, f32[]{:T(128)} %get-tuple-element.13), channel_id=1, replica_groups=mesh['gx'=16,'gy'=2] {'gy'}, use_global_device_ids=true, to_apply=%region_1.2 | all-reduce | flops 2 | bytes 16 | tf_op jit(solution)/shard_map/psum | solution.py:66
  27.3 30.1 %all-reduce.5 = (f32[]{:T(128)}, f32[]{:T(128)}) all-reduce(f32[]{:T(128)} %get-tuple-element.37, f32[]{:T(128)} %get-tuple-element.38), channel_id=1, replica_groups=mesh['gx'=16,'gy'=2] {'gx'}, use_global_device_ids=true, to_apply=%region_2.3 | all-reduce | flops 2 | bytes 16 | tf_op jit(solution)/shard_map/psum | solution.py:66
  58.9 4.4 %collective-permute-start.14 = (f32[128,1]{1,0:T(8,128)S(1)}, f32[128,1]{1,0:T(8,128)S(1)}, u32[]{:S(2)}, u32[]{:S(2)}) collective-permute-start(f32[128,1]{1,0:T(8,128)S(1)} %get-tuple-element.92), channel_id=1, source_target_pairs={{2,0},{4,2},{6,4},{8,6},{10,8},{12,10},{14,12},{16,14},{18,16},{20... | collective-permute-start | bytes 1544 | tf_op jit(solution)/shard_map/ppermute | solution.py:26
  63.3 1.9 collective-permute-done.13
  65.9 1.5 collective-permute-start.16
  67.4 1.5 collective-permute-done.15
  70.3 5.6 %all-reduce.10 = (f32[]{:T(128)}, f32[]{:T(128)}) all-reduce(f32[]{:T(128)} %get-tuple-element.12, f32[]{:T(128)} %get-tuple-element.11), channel_id=1, replica_groups=mesh['gx'=16,'gy'=2] {'gy'}, use_global_device_ids=true, to_apply=%region_7.8 | all-reduce | flops 2 | bytes 16 | tf_op jit(solution)/shard_map/psum | solution.py:66
  75.9 32.0 %all-reduce.4 = (f32[]{:T(128)}, f32[]{:T(128)}) all-reduce(f32[]{:T(128)} %get-tuple-element.35, f32[]{:T(128)} %get-tuple-element.36), channel_id=1, replica_groups=mesh['gx'=16,'gy'=2] {'gx'}, use_global_device_ids=true, to_apply=%region_8.9 | all-reduce | flops 2 | bytes 16 | tf_op jit(solution)/shard_map/psum | solution.py:66
  112.7 4.4 %collective-permute-start.18 = (f32[128,1]{1,0:T(8,128)S(1)}, f32[128,1]{1,0:T(8,128)S(1)}, u32[]{:S(2)}, u32[]{:S(2)}) collective-permute-start(f32[128,1]{1,0:T(8,128)S(1)} %get-tuple-element.90), channel_id=1, source_target_pairs={{2,0},{4,2},{6,4},{8,6},{10,8},{12,10},{14,12},{16,14},{18,16},{20... | collective-permute-start | bytes 1544 | tf_op jit(solution)/shard_map/ppermute | solution.py:26
  117.2 1.9 collective-permute-done.17
  119.2 1.5 collective-permute-start.19
  121.4 1.4 collective-permute-done.19
  122.7 1.5 collective-permute-done.20
  125.0 5.6 %all-reduce.9 = (f32[]{:T(128)}, f32[]{:T(128)}) all-reduce(f32[]{:T(128)} %get-tuple-element.10, f32[]{:T(128)} %get-tuple-element.9), channel_id=1, replica_groups=mesh['gx'=16,'gy'=2] {'gy'}, use_global_device_ids=true, to_apply=%region_13.14 | all-reduce | flops 2 | bytes 16 | tf_op jit(solution)/shard_map/psum | solution.py:66
  130.6 32.0 %all-reduce.3 = (f32[]{:T(128)}, f32[]{:T(128)}) all-reduce(f32[]{:T(128)} %get-tuple-element.33, f32[]{:T(128)} %get-tuple-element.34), channel_id=1, replica_groups=mesh['gx'=16,'gy'=2] {'gx'}, use_global_device_ids=true, to_apply=%region_14.15 | all-reduce | flops 2 | bytes 16 | tf_op jit(solution)/shard_map/psum | solution.py:66
  167.2 4.4 %collective-permute-start.22 = (f32[128,1]{1,0:T(8,128)}, f32[128,1]{1,0:T(8,128)S(1)}, u32[]{:S(2)}, u32[]{:S(2)}) collective-permute-start(f32[128,1]{1,0:T(8,128)} %get-tuple-element.88), channel_id=1, source_target_pairs={{2,0},{4,2},{6,4},{8,6},{10,8},{12,10},{14,12},{16,14},{18,16},{20... | collective-permute-start | bytes 1544 | tf_op jit(solution)/shard_map/ppermute | solution.py:26
  171.7 2.2 fusion.119
  173.9 2.0 copy.15
  176.4 4.4 %collective-permute-start.1 = (f32[3,8,128,1]{2,1,3,0:T(8,128)S(1)}, f32[3,8,128,1]{2,1,3,0:T(8,128)}, u32[]{:S(2)}, u32[]{:S(2)}) collective-permute-start(f32[3,8,128,1]{2,1,3,0:T(8,128)S(1)} %copy.16), channel_id=1, source_target_pairs={{2,0},{4,2},{6,4},{8,6},{10,8},{12,10},{14,12},{16,14},{18,16},{20... | collective-permute-start | bytes 36872 | tf_op jit(solution)/shard_map/ppermute | solution.py:26
  181.4 1.5 collective-permute-start.24
  183.0 1.5 collective-permute-done.23
  185.0 1.7 multiply_reduce_fusion.3
  186.7 5.6 %all-reduce.8 = (f32[]{:T(128)}, f32[]{:T(128)}) all-reduce(f32[]{:T(128)} %get-tuple-element.8, f32[]{:T(128)} %get-tuple-element.7), channel_id=1, replica_groups=mesh['gx'=16,'gy'=2] {'gy'}, use_global_device_ids=true, to_apply=%region_19.20 | all-reduce | flops 2 | bytes 16 | tf_op jit(solution)/shard_map/psum | solution.py:66
  192.3 30.2 %all-reduce.2 = (f32[]{:T(128)}, f32[]{:T(128)}) all-reduce(f32[]{:T(128)} %get-tuple-element.31, f32[]{:T(128)} %get-tuple-element.32), channel_id=1, replica_groups=mesh['gx'=16,'gy'=2] {'gx'}, use_global_device_ids=true, to_apply=%region_20.21 | all-reduce | flops 2 | bytes 16 | tf_op jit(solution)/shard_map/psum | solution.py:66
  226.6 4.4 %collective-permute-start.26 = (f32[128,1]{1,0:T(8,128)S(1)}, f32[128,1]{1,0:T(8,128)S(1)}, u32[]{:S(2)}, u32[]{:S(2)}) collective-permute-start(f32[128,1]{1,0:T(8,128)S(1)} %get-tuple-element.86), channel_id=1, source_target_pairs={{2,0},{4,2},{6,4},{8,6},{10,8},{12,10},{14,12},{16,14},{18,16},{20... | collective-permute-start | bytes 1544 | tf_op jit(solution)/shard_map/ppermute | solution.py:26
  231.0 1.9 collective-permute-done.25
  233.0 1.5 collective-permute-start.27
  236.6 1.5 collective-permute-done.28
  239.0 5.6 %all-reduce.7 = (f32[]{:T(128)}, f32[]{:T(128)}) all-reduce(f32[]{:T(128)} %get-tuple-element.6, f32[]{:T(128)} %get-tuple-element.5), channel_id=1, replica_groups=mesh['gx'=16,'gy'=2] {'gy'}, use_global_device_ids=true, to_apply=%region_25.26 | all-reduce | flops 2 | bytes 16 | tf_op jit(solution)/shard_map/psum | solution.py:66
  244.6 32.0 %all-reduce.1 = (f32[]{:T(128)}, f32[]{:T(128)}) all-reduce(f32[]{:T(128)} %get-tuple-element.29, f32[]{:T(128)} %get-tuple-element.30), channel_id=1, replica_groups=mesh['gx'=16,'gy'=2] {'gx'}, use_global_device_ids=true, to_apply=%region_26.27 | all-reduce | flops 2 | bytes 16 | tf_op jit(solution)/shard_map/psum | solution.py:66
  280.6 4.4 %collective-permute-start.30 = (f32[128,1]{1,0:T(8,128)S(1)}, f32[128,1]{1,0:T(8,128)S(1)}, u32[]{:S(2)}, u32[]{:S(2)}) collective-permute-start(f32[128,1]{1,0:T(8,128)S(1)} %get-tuple-element.84), channel_id=1, source_target_pairs={{2,0},{4,2},{6,4},{8,6},{10,8},{12,10},{14,12},{16,14},{18,16},{20... | collective-permute-start | bytes 1544 | tf_op jit(solution)/shard_map/ppermute | solution.py:26
  285.7 1.4 collective-permute-done.29
  288.3 1.4 collective-permute-start.32
  292.7 5.6 %all-reduce.6 = (f32[]{:T(128)}, f32[]{:T(128)}) all-reduce(f32[]{:T(128)} %get-tuple-element.4, f32[]{:T(128)} %get-tuple-element.3), channel_id=1, replica_groups=mesh['gx'=16,'gy'=2] {'gy'}, use_global_device_ids=true, to_apply=%region_31.32 | all-reduce | flops 2 | bytes 16 | tf_op jit(solution)/shard_map/psum | solution.py:66
  298.3 40.7 %all-reduce = (f32[]{:T(128)}, f32[]{:T(128)}) all-reduce(f32[]{:T(128)} %get-tuple-element.27, f32[]{:T(128)} %get-tuple-element.28), channel_id=1, replica_groups=mesh['gx'=16,'gy'=2] {'gx'}, use_global_device_ids=true, to_apply=%region_32.33 | all-reduce | flops 2 | bytes 16 | tf_op jit(solution)/shard_map/psum | solution.py:66
  343.6 3.1 collective-permute-start.33
  346.7 1.8 collective-permute-start.34
  348.6 1.9 collective-permute-done.33
  351.2 1.4 collective-permute-start.36
  356.2 1.4 collective-permute-start.3
  360.2 2.3 maximum_select_fusion
  363.7 3.3 bitcast_multiply_fusion
  (123 shorter events, 29.8 us)
Async XLA Ops:
  0.6 10.6 %copy-start.11 = (f32[128,128]{1,0:T(8,128)S(1)}, f32[128,128]{1,0:T(8,128)}, u32[]{:S(2)}) copy-start(f32[128,128]{1,0:T(8,128)} %param.17) | copy-start | bytes 196612
  0.6 7.9 %copy-start.14 = (f32[128,128]{1,0:T(8,128)S(1)}, f32[128,128]{1,0:T(8,128)}, u32[]{:S(2)}) copy-start(f32[128,128]{1,0:T(8,128)} %param.10) | copy-start | bytes 196612
  1.8 20.0 %copy-start.12 = (f32[8,128,128]{2,1,0:T(8,128)}, f32[8,128,128]{2,1,0:T(8,128)S(1)}, u32[]{:S(2)}) copy-start(f32[8,128,128]{2,1,0:T(8,128)S(1)} %convert_element_type.3) | copy-start | bytes 1572868
  2.9 8.3 %collective-permute-start.5 = (f32[2,128,1]{2,1,0:T(8,128)S(1)}, f32[2,128,1]{2,1,0:T(8,128)S(1)}, u32[]{:S(2)}, u32[]{:S(2)}) collective-permute-start(f32[2,128,1]{2,1,0:T(8,128)S(1)} %get-tuple-element.79), channel_id=1, source_target_pairs={{0,2},{2,4},{4,6},{6,8},{8,10},{10,12},{12,14},{14,16},{16,18},{18... | collective-permute-start | bytes 3080 | tf_op jit(solution)/shard_map/ppermute | solution.py:23
  3.5 7.7 %collective-permute-start.6 = (f32[2,128,1]{2,1,0:T(8,128)S(1)}, f32[2,128,1]{2,1,0:T(8,128)S(1)}, u32[]{:S(2)}, u32[]{:S(2)}) collective-permute-start(f32[2,128,1]{2,1,0:T(8,128)S(1)} %get-tuple-element.80), channel_id=1, source_target_pairs={{2,0},{4,2},{6,4},{8,6},{10,8},{12,10},{14,12},{16,14},{18,16},{20... | collective-permute-start | bytes 3080 | tf_op jit(solution)/shard_map/ppermute | solution.py:26
  8.6 4.8 %collective-permute-start.10 = (f32[128,1]{1,0:T(8,128)S(1)}, f32[128,1]{1,0:T(8,128)S(1)}, u32[]{:S(2)}, u32[]{:S(2)}) collective-permute-start(f32[128,1]{1,0:T(8,128)S(1)} %get-tuple-element.94), channel_id=1, source_target_pairs={{2,0},{4,2},{6,4},{8,6},{10,8},{12,10},{14,12},{16,14},{18,16},{20... | collective-permute-start | bytes 1544 | tf_op jit(solution)/shard_map/ppermute | solution.py:26
  9.3 6.4 %collective-permute-start.9 = (f32[128,1]{1,0:T(8,128)S(1)}, f32[128,1]{1,0:T(8,128)S(1)}, u32[]{:S(2)}, u32[]{:S(2)}) collective-permute-start(f32[128,1]{1,0:T(8,128)S(1)} %get-tuple-element.93), channel_id=1, source_target_pairs={{0,2},{2,4},{4,6},{6,8},{8,10},{10,12},{12,14},{14,16},{16,18},{18... | collective-permute-start | bytes 1544 | tf_op jit(solution)/shard_map/ppermute | solution.py:23
  11.3 6.5 %collective-permute-start.7 = (f32[2,1,130]{2,1,0:T(1,128)S(1)}, f32[2,1,130]{2,1,0:T(1,128)S(1)}, u32[]{:S(2)}, u32[]{:S(2)}) collective-permute-start(f32[2,1,130]{2,1,0:T(1,128)S(1)} %get-tuple-element.61), channel_id=1, source_target_pairs={{0,1},{1,0},{2,3},{3,2},{4,5},{5,4},{6,7},{7,6},{8,9},{9,8},{10,11... | collective-permute-start | bytes 3128 | tf_op jit(solution)/shard_map/ppermute | solution.py:23
  13.3 4.5 %collective-permute-start.8 = (f32[2,1,130]{2,1,0:T(1,128)S(1)}, f32[2,1,130]{2,1,0:T(1,128)S(1)}, u32[]{:S(2)}, u32[]{:S(2)}) collective-permute-start(f32[2,1,130]{2,1,0:T(1,128)S(1)} %get-tuple-element.62), channel_id=1, source_target_pairs={{1,0},{0,1},{3,2},{2,3},{5,4},{4,5},{7,6},{6,7},{9,8},{8,9},{11,10... | collective-permute-start | bytes 3128 | tf_op jit(solution)/shard_map/ppermute | solution.py:26
  15.8 3.6 collective-permute-start.11
  17.3 3.6 collective-permute-start.12
  18.0 99.1 %copy-start.7 = (s32[8,128,128]{2,1,0:T(8,128)S(1)}, s32[8,128,128]{2,1,0:T(8,128)}, u32[]{:S(2)}) copy-start(s32[8,128,128]{2,1,0:T(8,128)} %param.16) | copy-start | bytes 1572868
  18.0 99.1 %copy-start.9 = (f32[8,128,128]{2,1,0:T(8,128)S(1)}, f32[8,128,128]{2,1,0:T(8,128)}, u32[]{:S(2)}) copy-start(f32[8,128,128]{2,1,0:T(8,128)} %param.9) | copy-start | bytes 1572868
  58.8 62.4 %copy-start = (f32[8,128,128]{2,1,0:T(8,128)S(1)}, f32[8,128,128]{2,1,0:T(8,128)}, u32[]{:S(2)}) copy-start(f32[8,128,128]{2,1,0:T(8,128)} %param.12) | copy-start | bytes 1572868
  58.8 62.4 %copy-start.2 = (f32[8,128,128]{2,1,0:T(8,128)S(1)}, f32[8,128,128]{2,1,0:T(8,128)}, u32[]{:S(2)}) copy-start(f32[8,128,128]{2,1,0:T(8,128)} %param.11) | copy-start | bytes 1572868
  58.8 6.4 %collective-permute-start.13 = (f32[128,1]{1,0:T(8,128)S(1)}, f32[128,1]{1,0:T(8,128)S(1)}, u32[]{:S(2)}, u32[]{:S(2)}) collective-permute-start(f32[128,1]{1,0:T(8,128)S(1)} %get-tuple-element.91), channel_id=1, source_target_pairs={{0,2},{2,4},{4,6},{6,8},{8,10},{10,12},{12,14},{14,16},{16,18},{18... | collective-permute-start | bytes 1544 | tf_op jit(solution)/shard_map/ppermute | solution.py:23
  58.9 6.4 %collective-permute-start.14 = (f32[128,1]{1,0:T(8,128)S(1)}, f32[128,1]{1,0:T(8,128)S(1)}, u32[]{:S(2)}, u32[]{:S(2)}) collective-permute-start(f32[128,1]{1,0:T(8,128)S(1)} %get-tuple-element.92), channel_id=1, source_target_pairs={{2,0},{4,2},{6,4},{8,6},{10,8},{12,10},{14,12},{16,14},{18,16},{20... | collective-permute-start | bytes 1544 | tf_op jit(solution)/shard_map/ppermute | solution.py:26
  65.4 3.6 collective-permute-start.15
  65.9 3.6 collective-permute-start.16
  112.7 6.4 %collective-permute-start.17 = (f32[128,1]{1,0:T(8,128)S(1)}, f32[128,1]{1,0:T(8,128)S(1)}, u32[]{:S(2)}, u32[]{:S(2)}) collective-permute-start(f32[128,1]{1,0:T(8,128)S(1)} %get-tuple-element.89), channel_id=1, source_target_pairs={{0,2},{2,4},{4,6},{6,8},{8,10},{10,12},{12,14},{14,16},{16,18},{18... | collective-permute-start | bytes 1544 | tf_op jit(solution)/shard_map/ppermute | solution.py:23
  112.7 6.4 %collective-permute-start.18 = (f32[128,1]{1,0:T(8,128)S(1)}, f32[128,1]{1,0:T(8,128)S(1)}, u32[]{:S(2)}, u32[]{:S(2)}) collective-permute-start(f32[128,1]{1,0:T(8,128)S(1)} %get-tuple-element.90), channel_id=1, source_target_pairs={{2,0},{4,2},{6,4},{8,6},{10,8},{12,10},{14,12},{16,14},{18,16},{20... | collective-permute-start | bytes 1544 | tf_op jit(solution)/shard_map/ppermute | solution.py:26
  119.2 3.6 collective-permute-start.19
  120.7 3.6 collective-permute-start.20
  167.2 13.6 %collective-permute-start.21 = (f32[128,1]{1,0:T(8,128)}, f32[128,1]{1,0:T(8,128)S(1)}, u32[]{:S(2)}, u32[]{:S(2)}) collective-permute-start(f32[128,1]{1,0:T(8,128)} %get-tuple-element.87), channel_id=1, source_target_pairs={{0,2},{2,4},{4,6},{6,8},{8,10},{10,12},{12,14},{14,16},{16,18},{18... | collective-permute-start | bytes 1544 | tf_op jit(solution)/shard_map/ppermute | solution.py:23
  167.2 13.6 %collective-permute-start.22 = (f32[128,1]{1,0:T(8,128)}, f32[128,1]{1,0:T(8,128)S(1)}, u32[]{:S(2)}, u32[]{:S(2)}) collective-permute-start(f32[128,1]{1,0:T(8,128)} %get-tuple-element.88), channel_id=1, source_target_pairs={{2,0},{4,2},{6,4},{8,6},{10,8},{12,10},{14,12},{16,14},{18,16},{20... | collective-permute-start | bytes 1544 | tf_op jit(solution)/shard_map/ppermute | solution.py:26
  173.9 9.1 %copy-start.15 = (s32[1,1,8]{2,1,0:T(1,128)S(1)}, s32[1,1,8]{2,1,0:T(1,128)}, u32[]{:S(2)}) copy-start(s32[1,1,8]{2,1,0:T(1,128)} %param.15) | copy-start | bytes 100
  175.9 176.7 %collective-permute-start = (f32[3,8,128,1]{2,1,3,0:T(8,128)S(1)}, f32[3,8,128,1]{2,1,3,0:T(8,128)S(1)}, u32[]{:S(2)}, u32[]{:S(2)}) collective-permute-start(f32[3,8,128,1]{2,1,3,0:T(8,128)S(1)} %copy.15), channel_id=1, source_target_pairs={{0,2},{2,4},{4,6},{6,8},{8,10},{10,12},{12,14},{14,16},{16,18},{18... | collective-permute-start | bytes 36872 | tf_op jit(solution)/shard_map/ppermute | solution.py:23
  176.4 176.7 %collective-permute-start.1 = (f32[3,8,128,1]{2,1,3,0:T(8,128)S(1)}, f32[3,8,128,1]{2,1,3,0:T(8,128)}, u32[]{:S(2)}, u32[]{:S(2)}) collective-permute-start(f32[3,8,128,1]{2,1,3,0:T(8,128)S(1)} %copy.16), channel_id=1, source_target_pairs={{2,0},{4,2},{6,4},{8,6},{10,8},{12,10},{14,12},{16,14},{18,16},{20... | collective-permute-start | bytes 36872 | tf_op jit(solution)/shard_map/ppermute | solution.py:26
  180.9 3.6 collective-permute-start.23
  181.4 3.6 collective-permute-start.24
  226.6 6.4 %collective-permute-start.25 = (f32[128,1]{1,0:T(8,128)S(1)}, f32[128,1]{1,0:T(8,128)S(1)}, u32[]{:S(2)}, u32[]{:S(2)}) collective-permute-start(f32[128,1]{1,0:T(8,128)S(1)} %get-tuple-element.85), channel_id=1, source_target_pairs={{0,2},{2,4},{4,6},{6,8},{8,10},{10,12},{12,14},{14,16},{16,18},{18... | collective-permute-start | bytes 1544 | tf_op jit(solution)/shard_map/ppermute | solution.py:23
  226.6 6.4 %collective-permute-start.26 = (f32[128,1]{1,0:T(8,128)S(1)}, f32[128,1]{1,0:T(8,128)S(1)}, u32[]{:S(2)}, u32[]{:S(2)}) collective-permute-start(f32[128,1]{1,0:T(8,128)S(1)} %get-tuple-element.86), channel_id=1, source_target_pairs={{2,0},{4,2},{6,4},{8,6},{10,8},{12,10},{14,12},{16,14},{18,16},{20... | collective-permute-start | bytes 1544 | tf_op jit(solution)/shard_map/ppermute | solution.py:26
  233.0 3.6 collective-permute-start.27
  234.6 3.6 collective-permute-start.28
  280.6 6.5 %collective-permute-start.29 = (f32[128,1]{1,0:T(8,128)S(1)}, f32[128,1]{1,0:T(8,128)S(1)}, u32[]{:S(2)}, u32[]{:S(2)}) collective-permute-start(f32[128,1]{1,0:T(8,128)S(1)} %get-tuple-element.83), channel_id=1, source_target_pairs={{0,2},{2,4},{4,6},{6,8},{8,10},{10,12},{12,14},{14,16},{16,18},{18... | collective-permute-start | bytes 1544 | tf_op jit(solution)/shard_map/ppermute | solution.py:23
  280.6 7.0 %collective-permute-start.30 = (f32[128,1]{1,0:T(8,128)S(1)}, f32[128,1]{1,0:T(8,128)S(1)}, u32[]{:S(2)}, u32[]{:S(2)}) collective-permute-start(f32[128,1]{1,0:T(8,128)S(1)} %get-tuple-element.84), channel_id=1, source_target_pairs={{2,0},{4,2},{6,4},{8,6},{10,8},{12,10},{14,12},{16,14},{18,16},{20... | collective-permute-start | bytes 1544 | tf_op jit(solution)/shard_map/ppermute | solution.py:26
  287.7 3.6 collective-permute-start.31
  288.3 3.6 collective-permute-start.32
  290.9 71.9 %collective-permute-start.4 = (f32[2,8,128,128]{3,2,0,1:T(8,128)}, f32[2,8,128,128]{3,2,0,1:T(8,128)}, u32[]{:S(2)}, u32[]{:S(2)}) collective-permute-start(f32[2,8,128,128]{3,2,0,1:T(8,128)} %select_bitcast_fusion), channel_id=1, source_target_pairs={{0,16},{2,18},{4,20},{6,22},{8,24},{10,26},{12,28},{14,30},{16,0},... | collective-permute-start | bytes 3145736 | tf_op jit(solution)/shard_map/ppermute | solution.py:34
  343.6 6.8 %collective-permute-start.33 = (f32[128,1]{1,0:T(8,128)S(1)}, f32[128,1]{1,0:T(8,128)S(1)}, u32[]{:S(2)}, u32[]{:S(2)}) collective-permute-start(f32[128,1]{1,0:T(8,128)S(1)} %get-tuple-element.81), channel_id=1, source_target_pairs={{0,2},{2,4},{4,6},{6,8},{8,10},{10,12},{12,14},{14,16},{16,18},{18... | collective-permute-start | bytes 1544 | tf_op jit(solution)/shard_map/ppermute | solution.py:23
  346.7 3.7 %collective-permute-start.34 = (f32[128,1]{1,0:T(8,128)S(1)}, f32[128,1]{1,0:T(8,128)S(1)}, u32[]{:S(2)}, u32[]{:S(2)}) collective-permute-start(f32[128,1]{1,0:T(8,128)S(1)} %get-tuple-element.82), channel_id=1, source_target_pairs={{2,0},{4,2},{6,4},{8,6},{10,8},{12,10},{14,12},{16,14},{18,16},{20... | collective-permute-start | bytes 1544 | tf_op jit(solution)/shard_map/ppermute | solution.py:26
  350.5 7.1 %collective-permute-start.35 = (f32[1,130]{1,0:T(1,128)S(1)}, f32[1,130]{1,0:T(1,128)S(1)}, u32[]{:S(2)}, u32[]{:S(2)}) collective-permute-start(f32[1,130]{1,0:T(1,128)S(1)} %get-tuple-element.65), channel_id=1, source_target_pairs={{0,1},{1,0},{2,3},{3,2},{4,5},{5,4},{6,7},{7,6},{8,9},{9,8},{10,11... | collective-permute-start | bytes 1568 | tf_op jit(solution)/shard_map/ppermute | solution.py:23
  351.2 6.4 %collective-permute-start.36 = (f32[1,130]{1,0:T(1,128)S(1)}, f32[1,130]{1,0:T(1,128)S(1)}, u32[]{:S(2)}, u32[]{:S(2)}) collective-permute-start(f32[1,130]{1,0:T(1,128)S(1)} %get-tuple-element.66), channel_id=1, source_target_pairs={{1,0},{0,1},{3,2},{2,3},{5,4},{4,5},{7,6},{6,7},{9,8},{8,9},{11,10... | collective-permute-start | bytes 1568 | tf_op jit(solution)/shard_map/ppermute | solution.py:26
  354.3 5.9 %copy-start.1 = (f32[8,128,128]{2,1,0:T(8,128)S(1)}, f32[8,128,128]{2,1,0:T(8,128)}, u32[]{:S(2)}) copy-start(f32[8,128,128]{2,1,0:T(8,128)} %param.12) | copy-start | bytes 1572868
  354.3 5.9 %copy-start.3 = (f32[8,128,128]{2,1,0:T(8,128)S(1)}, f32[8,128,128]{2,1,0:T(8,128)}, u32[]{:S(2)}) copy-start(f32[8,128,128]{2,1,0:T(8,128)} %param.11) | copy-start | bytes 1572868
  354.3 5.9 %copy-start.5 = (f32[1,8,128,128]{3,2,1,0:T(8,128)S(1)}, f32[1,8,128,128]{3,2,1,0:T(8,128)}, u32[]{:S(2)}) copy-start(f32[1,8,128,128]{3,2,1,0:T(8,128)} %copy-done.4) | copy-start | bytes 1572868
  355.5 3.9 %collective-permute-start.2 = (f32[3,8,1,130]{3,2,1,0:T(1,128)S(1)}, f32[3,8,1,130]{3,2,1,0:T(1,128)S(1)}, u32[]{:S(2)}, u32[]{:S(2)}) collective-permute-start(f32[3,8,1,130]{3,2,1,0:T(1,128)S(1)} %get-tuple-element.52), channel_id=1, source_target_pairs={{0,1},{1,0},{2,3},{3,2},{4,5},{5,4},{6,7},{7,6},{8,9},{9,8},{10,11... | collective-permute-start | bytes 37448 | tf_op jit(solution)/shard_map/ppermute | solution.py:23
  356.2 4.0 %collective-permute-start.3 = (f32[3,8,1,130]{3,2,1,0:T(1,128)S(1)}, f32[3,8,1,130]{3,2,1,0:T(1,128)S(1)}, u32[]{:S(2)}, u32[]{:S(2)}) collective-permute-start(f32[3,8,1,130]{3,2,1,0:T(1,128)S(1)} %get-tuple-element.53), channel_id=1, source_target_pairs={{1,0},{0,1},{3,2},{2,3},{5,4},{4,5},{7,6},{6,7},{9,8},{8,9},{11,10... | collective-permute-start | bytes 37448 | tf_op jit(solution)/shard_map/ppermute | solution.py:26
  (5 other events, 12.1 us)
